TPU v7x, 32 devices: a whole 2x2x4 slice. The times are simulated.
32 devices in a mesh: dp: 16 (over z, y, x), mp: 2 (over core).
Axes of the slice: x: 2, y: 2, z: 4, core: 2. Of those that a mesh axis runs over, the one named last changes fastest.
Arguments:
- attn: bfloat16 [6144, 1536], P('dp', 'mp'), may hold values from -6 to 6
- w_out: bfloat16 [1536, 1536], P('mp'), may hold values from -0.15625 to 0.15625
- resid: bfloat16 [6144, 1536], P('dp', 'mp'), may hold values from -6 to 6
- target: bfloat16 [6144, 1536], P('dp', 'mp'), may hold values from -6 to 6
- gate: float32 [48, 1536], P('dp', 'mp'), may hold values from -5 to 5
- bins: int32 [48], P('dp'), may hold values from 0 to 127
Outputs:
- grad_w_out: float32 [1536, 1536], P('dp', 'mp')
- grad_gate: float32 [48, 1536], P('dp', 'mp')
- bin_loss: float32 [128], replicated
All inputs are finite; a program needn't handle non-finite values.
Results may differ from a plain program's by a relative error of at most 0.0008.
Values may be sent and summed in bfloat16 or wider, within the bound.
A program may use at most 64 MiB of HBM per device.

v0:
```python
import math

import jax
import jax.numpy as jnp
from jax import lax
from jax.sharding import PartitionSpec as P

NBINS = 128


LOSS_SCALE = 4096.0


def bin_weights():
    centre = (jnp.arange(NBINS).astype(jnp.float32) + 0.5) / NBINS
    logit = jnp.log(centre) - jnp.log(1.0 - centre)
    return jnp.exp(-0.5 * logit * logit) / (math.sqrt(2.0 * math.pi) * centre * (1.0 - centre))


def shards(attn, w_out, resid, target, gate, bins):
    samples = bins.shape[0]
    tok_rows = attn.shape[0]
    per_sample = tok_rows // samples
    full_width = w_out.shape[1]
    own_cols = resid.shape[1]
    bin_ids = jnp.arange(NBINS, dtype=jnp.int32)
    one_hot = (bins[:, None] == bin_ids[None, :]).astype(jnp.float32)
    local_counts = jnp.sum(one_hot, axis=0)
    weights = bin_weights()
    counts = lax.psum(local_counts, "dp")
    whole_attn = lax.all_gather(attn, "mp", axis=1, tiled=True)
    partial_value = jnp.dot(attn, w_out, preferred_element_type=jnp.float32)
    projected = lax.psum_scatter(partial_value, "mp", scatter_dimension=1, tiled=True)
    proj_cube = projected.reshape(samples, per_sample, own_cols)
    hidden = (
        resid.reshape(samples, per_sample, own_cols).astype(jnp.float32)
        + gate[:, None, :] * proj_cube
    )
    error_cube = hidden - target.reshape(samples, per_sample, own_cols).astype(jnp.float32)
    sample_error = jnp.sum(error_cube * error_cube, axis=(1, 2)) / (per_sample * full_width)
    bin_part = jnp.sum(one_hot * sample_error[:, None], axis=0)
    sums = lax.psum(bin_part, ("dp", "mp"))
    floored = jnp.maximum(counts, 1.0)
    scale_bin = LOSS_SCALE * weights / floored
    coefficient = jnp.sum(one_hot * scale_bin[None, :], axis=1) * (2.0 / (per_sample * full_width))
    d_hidden = coefficient[:, None, None] * error_cube
    grad_gate = jnp.sum(d_hidden * proj_cube, axis=1)
    d_proj = (d_hidden * gate[:, None, :]).astype(jnp.bfloat16).reshape(tok_rows, own_cols)
    full_grad = lax.dot_general(
        whole_attn, d_proj, (((0,), (0,)), ((), ())), preferred_element_type=jnp.float32
    )
    grad_out = lax.psum_scatter(full_grad, "dp", scatter_dimension=0, tiled=True)
    bin_loss = weights * sums / floored
    return (grad_out, grad_gate, bin_loss)


def solution(mesh):
    return jax.shard_map(
        shards,
        mesh=mesh,
        in_specs=(
            P("dp", "mp"),
            P("mp", None),
            P("dp", "mp"),
            P("dp", "mp"),
            P("dp", "mp"),
            P("dp"),
        ),
        out_specs=(P("dp", "mp"), P("dp", "mp"), P()),
        check_vma=False,
    )
```

profile of v0, /device:TPU:0, one launch (start us, length us, event | category | flops | bytes accessed | tf_op | source)
XLA Modules:
  0.0 214.0 jit_solution(4137970757654208983)
XLA Ops:
  7.2 0.0 copy-start
  7.2 0.0 reduce-scatter.5.cloned.1.call-start
  7.2 1.6 copy-done
  8.8 3.6 %fusion.5 = f32[384,1536]{1,0:T(8,128)} fusion(bf16[384,768]{1,0:T(8,128)(2,1)} %param.6, bf16[768,1536]{1,0:T(8,128)(2,1)S(1)} %copy-done), kind=kOutput, calls=%fused_computation.21 | convolution fusion | flops 905969664 | bytes 5308416 | tf_op jit(solution)/shard_map/dot_general | solution.py:32
  12.4 0.0 copy-start.5
  12.4 0.0 copy-start.4
  12.4 0.0 reduce-scatter.5.cloned.1.call-update
  12.4 0.0 all-gather.2.cloned.1.call-start
  12.5 0.7 all-gather.2.cloned.1.call-update
  13.2 0.0 reduce-scatter.7.cloned.1.call-start
  13.2 0.0 copy-done.5
  13.2 0.1 convert_reduce_fusion
  13.3 43.5 %psum.14 = f32[128]{0:T(128)S(1)} all-reduce(f32[128]{0:T(128)S(1)} %convert_reduce_fusion), channel_id=1, replica_groups=mesh['dp'=16,'mp'=2] {'dp'}, use_global_device_ids=true, to_apply=%region_1.0 | all-reduce | flops 128 | bytes 1024 | tf_op jit(solution)/shard_map/psum | solution.py:30
  56.8 0.0 copy-start.7
  56.8 0.5 multiply_divide_fusion.1
  57.4 0.0 copy-done.7
  57.4 0.0 reduce-scatter.5.cloned.1.call-done
  57.4 0.0 copy-done.4
  57.4 0.0 copy-start.6
  57.4 0.0 copy-start.1
  57.4 0.0 copy-start.2
  57.4 0.0 copy-start.3
  57.4 2.1 multiply_reduce_fusion
  59.5 0.1 bitcast_reduce_fusion
  59.6 0.0 copy-done.6
  59.6 0.6 select_reduce_fusion
  60.2 0.1 broadcast_bitcast_fusion
  60.3 0.0 copy-done.1
  60.3 0.0 copy-done.2
  60.3 0.0 copy-done.3
  60.3 1.1 fusion.2
  61.4 0.0 all-gather.2.cloned.1.call-done
  61.4 5.0 %convolution_bitcast_fusion = f32[1536,768]{0,1:T(8,128)} fusion(bf16[384,768]{1,0:T(8,128)(2,1)} %fusion.2, bf16[384,1536]{1,0:T(8,128)(2,1)} %all-gather.2.cloned.1.call-done), kind=kOutput, calls=%fused_computation | convolution fusion | flops 905969664 | bytes 6488064 | tf_op jit(solution)/shard_map/dot_general | solution.py:49
  66.4 6.1 %copy.12 = f32[1536,768]{1,0:T(8,128)} copy(f32[1536,768]{0,1:T(8,128)} %convolution_bitcast_fusion) | data formatting | bytes 9437184
  72.6 0.0 reduce-scatter.7.cloned.1.call-update
  72.6 37.9 %psum.15 = f32[128]{0:T(128)} all-reduce(f32[128]{0:T(128)} %get-tuple-element.12), channel_id=1, replica_groups=mesh['dp'=16,'mp'=2] {'dp','mp'}, use_global_device_ids=true, to_apply=%region_9.10 | all-reduce | flops 128 | bytes 1024 | tf_op jit(solution)/shard_map/psum | solution.py:42
  110.5 1.2 multiply_divide_fusion
  111.7 2.2 %multiply_reduce_fusion.1 = f32[3,768]{1,0:T(4,128)} fusion(f32[3,128,768]{2,1,0:T(8,128)S(1)} %bitcast.29, f32[3]{0:T(128)S(1)} %broadcast_multiply_fusion.1, f32[3,768]{1,0:T(4,128)S(1)} %copy-done.4, bf16[3,128,768]{2,1,0:T(8,128)(2,1)} %bitcast.31, bf16[3,128,768]{2,1,0:T(8,128)(2,1)} %bitcast.30), kind=kLoop, calls=%fused_computation.7 | loop fusion | flops 2356992 | bytes 2377740 | tf_op jit(solution)/shard_map/reduce_sum | solution.py:47
  113.9 93.5 %reduce-scatter.7.cloned.1.call-done = f32[96,768]{1,0:T(8,128)} async-done(((f32[1536,768]{1,0:T(8,128)}), f32[96,768]{1,0:T(8,128)}) %reduce-scatter.7.cloned.1.call-update) | async-done | bytes 294928
  (2 shorter events, 0.0 us)
Async XLA Ops:
  7.2 1.7 copy-start
  7.2 50.2 %reduce-scatter.5.cloned.1.call-start = ((), (), s32[]{:S(2)}) async-start(), calls=%async_computation.2 | async-start | bytes 3538944 | tf_op jit(solution)/shard_map/reduce_scatter | solution.py:33
  12.4 0.8 copy-start.5
  12.4 45.0 %copy-start.4 = (f32[3,768]{1,0:T(4,128)S(1)}, f32[3,768]{1,0:T(4,128)}, u32[]{:S(2)}) copy-start(f32[3,768]{1,0:T(4,128)} %param.10) | copy-start | bytes 27652
  12.4 49.0 %all-gather.2.cloned.1.call-start = ((), (), s32[]{:S(2)}) async-start(), calls=%async_computation.3 | async-start | bytes 1769472 | tf_op jit(solution)/shard_map/all_gather | solution.py:31
  13.2 194.3 %reduce-scatter.7.cloned.1.call-start = ((), (), s32[]{:S(2)}) async-start(), calls=%async_computation.4 | async-start | bytes 5013504
  56.8 0.5 copy-start.7
  57.4 2.3 %copy-start.6 = (f32[128]{0:T(128)S(1)}, f32[128]{0:T(128)}, u32[]{:S(2)}) copy-start(f32[128]{0:T(128)} %multiply_divide_fusion.1) | copy-start | bytes 1540
  57.4 2.9 %copy-start.1 = (f32[384,768]{1,0:T(8,128)S(1)}, f32[384,768]{1,0:T(8,128)}, u32[]{:S(2)}) copy-start(f32[384,768]{1,0:T(8,128)} %reduce-scatter.5.cloned.1.call-done) | copy-start | bytes 3538948
  57.4 2.9 %copy-start.2 = (bf16[384,768]{1,0:T(8,128)(2,1)S(1)}, bf16[384,768]{1,0:T(8,128)(2,1)}, u32[]{:S(2)}) copy-start(bf16[384,768]{1,0:T(8,128)(2,1)} %param.9) | copy-start | bytes 1769476
  57.4 2.9 %copy-start.3 = (bf16[384,768]{1,0:T(8,128)(2,1)S(1)}, bf16[384,768]{1,0:T(8,128)(2,1)}, u32[]{:S(2)}) copy-start(bf16[384,768]{1,0:T(8,128)(2,1)} %param.8) | copy-start | bytes 1769476
Sparse Core Ops, SparseCore 0:
  12.5 12.7 reduce-scatter.4
  26.8 10.5 all-gather.1
  72.7 134.7 reduce-scatter.6
where the time goes:
time: 214 us
  waiting for transfers between devices  94.3 us (44%)
  blocking collectives  81.4 us (38%)
  between operations  13.8 us (6%)
  matrix products  8.55 us (4%)
  other arithmetic  7.99 us (4%)
  local copies, waits for them, and re-layouts  7.85 us (4%)
    unnamed x4, waiting for transfers between devices  94.3 us
    psum x1, blocking collectives, shards(): counts = lax.psum(local_counts, 'dp')  43.5 us
    psum x1, blocking collectives, shards(): sums = lax.psum(bin_part, ('dp', 'mp'))  37.9 us
    unnamed x17, local copies, waits for them, and re-layouts  7.78 us
    dot_general x1, matrix products, shards(): lax.dot_general(whole_attn, d_proj, (((0,), (0,)), ((), ())), preferred_e...  4.99 us
  transfers between devices with their start and end apart: 3, of which 1 were waited for; matrix products, arithmetic and copies ran while one was open for 4% of the time, Pallas kernels for 0%

commit v1 on v0

--- a/solution.py
+++ b/solution.py
@@ -1,8 +1,11 @@
+import functools
 import math
 
 import jax
 import jax.numpy as jnp
 from jax import lax
+from jax.experimental import pallas as pl
+from jax.experimental.pallas import tpu as pltpu
 from jax.sharding import PartitionSpec as P
 
 NBINS = 128
@@ -54,9 +57,325 @@
     return (grad_out, grad_gate, bin_loss)
 
 
+MESH = pl.DeviceIdType.MESH
+LANES = 128
+PLANE = 4
+
+
+def fused_kernel(
+    n, full_width,
+    attn_h, w_h, resid_h, target_h, gate_ref, bins_ref,
+    grad_ref, gg_ref, loss_ref,
+    attn_v, w_v, resid_v, target_v, err, psend, precv,
+    at_send, at, dp, gbuf, ra, sb, rb, cnt, lpart, lbuf,
+    ld, fs, fr, a_s, a_r, p_s, p_r, c_s, c_r, l_s, l_r, lp_s, lp_r,
+    dx_s, dx_r, dy_s, dy_r, fx_s, fx_r, fy_s, fy_r, za_s, za_r, zb_s, zb_r,
+):
+    d = lax.axis_index("dp")
+    mp = lax.axis_index("mp")
+    other = 1 - mp
+    x = lax.rem(d, 2)
+    y = lax.rem(lax.div(d, 2), 2)
+    q = lax.rem(d, PLANE)
+    b0 = lax.rem(lax.div(d, PLANE), 2)
+    b1 = lax.div(d, 2 * PLANE)
+    x_q = q + 1 - 2 * x
+    y_q = q + 2 - 4 * y
+    xy_q = x_q + 2 - 4 * y
+    base = d - q
+    x_dev, y_dev, xy_dev = (base + x_q, mp), (base + y_q, mp), (base + xy_q, mp)
+    za_dev = (d + PLANE - 2 * PLANE * b0, mp)
+    zb_dev = (d + 2 * PLANE - 4 * PLANE * b1, mp)
+    partner = (d, other)
+
+    rows, own_cols = attn_v.shape
+    samples = gate_ref.shape[0]
+    tok = rows // samples
+    nb = dp.shape[1]
+    nf, _, fw = psend.shape
+    chunk = grad_ref.shape[0]
+    half = rows // 2
+
+    def remote(src, dst, send, recv, dev):
+        return pltpu.make_async_remote_copy(
+            src_ref=src, dst_ref=dst, send_sem=send, recv_sem=recv, device_id=dev, device_id_type=MESH
+        )
+
+    def own_half(which):
+        return w_h.at[:, pl.ds(pl.multiple_of(which * own_cols, LANES), own_cols)]
+
+    loads = [
+        pltpu.make_async_copy(attn_h, attn_v, ld.at[0]),
+        pltpu.make_async_copy(own_half(other), w_v.at[0], ld.at[1]),
+        pltpu.make_async_copy(own_half(mp), w_v.at[1], ld.at[2]),
+        pltpu.make_async_copy(resid_h, resid_v, ld.at[3]),
+        pltpu.make_async_copy(target_h, target_v, ld.at[4]),
+    ]
+    for load in loads:
+        load.start()
+
+    barrier = pltpu.get_barrier_semaphore()
+    for k in range(1, n):
+        pl.semaphore_signal(barrier, inc=1, device_id=(lax.rem(d + k, n), mp), device_id_type=MESH)
+    pl.semaphore_signal(barrier, inc=1, device_id=partner, device_id_type=MESH)
+
+    lane = lax.broadcasted_iota(jnp.int32, (8, LANES), 1)
+    one_hot = [(lane == bins_ref[s]).astype(jnp.float32) for s in range(samples)]
+    counts_own = one_hot[0]
+    for s in range(1, samples):
+        counts_own = counts_own + one_hot[s]
+    cnt[d] = counts_own
+
+    loads[0].wait()
+    turned = attn_v[...].T
+    for k in range(own_cols // chunk):
+        zz, to = k // PLANE, k % PLANE
+        at_send[to, zz * chunk:(zz + 1) * chunk, :] = turned[k * chunk:(k + 1) * chunk]
+
+    pl.semaphore_wait(barrier, n)
+
+    count_copies = []
+    for k in range(1, n):
+        copy = remote(cnt.at[d], cnt.at[d], c_s.at[k], c_r.at[k], (lax.rem(d + k, n), mp))
+        copy.start()
+        count_copies.append(copy)
+    attn_copies = []
+    for r, (peer_q, dev) in enumerate(((xy_q, xy_dev), (x_q, x_dev), (y_q, y_dev))):
+        copy = remote(at_send.at[peer_q], at.at[q, mp], a_s.at[r], a_r.at[r], dev)
+        copy.start()
+        attn_copies.append(copy)
+    partner_copies = [remote(at_send.at[q], at.at[q, mp], p_s.at[3], p_r.at[3], partner)]
+    partner_copies[0].start()
+    at[q, mp] = at_send[q]
+
+    loads[1].wait()
+    part_copies = []
+    for j in range(nf):
+        cols = slice(j * fw, (j + 1) * fw)
+        psend[j] = jnp.dot(attn_v[...], w_v[0, :, cols], preferred_element_type=jnp.float32)
+        copy = remote(psend.at[j], precv.at[j], fs.at[j], fr.at[j], partner)
+        copy.start()
+        part_copies.append(copy)
+    loads[2].wait()
+    loads[3].wait()
+    loads[4].wait()
+    square = [jnp.zeros((1, fw), jnp.float32) for _ in range(samples)]
+    gate_sums = []
+    for j in range(nf):
+        cols = slice(j * fw, (j + 1) * fw)
+        own = jnp.dot(attn_v[...], w_v[1, :, cols], preferred_element_type=jnp.float32)
+        part_copies[j].wait_recv()
+        sums = []
+        for s in range(samples):
+            toks = slice(s * tok, (s + 1) * tok)
+            proj = own[toks] + precv[j, toks, :]
+            gate = gate_ref[s:s + 1, cols]
+            hidden = resid_v[toks, cols].astype(jnp.float32) + gate * proj
+            error = hidden - target_v[toks, cols].astype(jnp.float32)
+            err[toks, cols] = error
+            square[s] = square[s] + jnp.sum(error * error, axis=0, keepdims=True)
+            sums.append(jnp.sum(error * proj, axis=0, keepdims=True))
+        gate_sums.append(sums)
+
+    bin_part = jnp.zeros((8, LANES), jnp.float32)
+    for s in range(samples):
+        sample_error = jnp.sum(square[s], axis=1, keepdims=True) / (tok * full_width)
+        bin_part = bin_part + one_hot[s] * sample_error
+    lpart[mp] = bin_part
+    loss_pair = remote(lpart.at[mp], lpart.at[mp], lp_s.at[0], lp_r.at[0], partner)
+    loss_pair.start()
+
+    centre = (lane.astype(jnp.float32) + 0.5) / LANES
+    logit = jnp.log(centre) - jnp.log(1.0 - centre)
+    weights = jnp.exp(-0.5 * logit * logit) / (math.sqrt(2.0 * math.pi) * centre * (1.0 - centre))
+
+    for copy in count_copies:
+        copy.wait_recv()
+    counts = cnt[0]
+    for k in range(1, n):
+        counts = counts + cnt[k]
+    floored = jnp.maximum(counts, 1.0)
+    scale_bin = LOSS_SCALE * weights / floored
+    coef = [
+        jnp.sum((one_hot[s] * scale_bin)[0:1], axis=1, keepdims=True) * (2.0 / (tok * full_width))
+        for s in range(samples)
+    ]
+
+    def make_d_proj(c):
+        cols = slice(c * LANES, (c + 1) * LANES)
+        for s in range(samples):
+            toks = slice(s * tok, (s + 1) * tok)
+            d_hidden = coef[s] * err[toks, cols]
+            dp[q, c, toks, :] = (d_hidden * gate_ref[s:s + 1, cols]).astype(jnp.bfloat16)
+
+    direct_x = [remote(dp.at[q, c], dp.at[q, c], dx_s.at[c], dx_r.at[c], x_dev) for c in range(nb)]
+    direct_y = [remote(dp.at[q, c], dp.at[q, c], dy_s.at[c], dy_r.at[c], y_dev) for c in range(nb)]
+    first, second = pl.ds(0, half), pl.ds(half, half)
+    pass_y = [
+        remote(dp.at[x_q, c, first], dp.at[x_q, c, first], fy_s.at[c], fy_r.at[c], y_dev)
+        for c in range(nb)
+    ]
+    pass_x = [
+        remote(dp.at[y_q, c, second], dp.at[y_q, c, second], fx_s.at[c], fx_r.at[c], x_dev)
+        for c in range(nb)
+    ]
+    halve_a = [remote(gbuf.at[c, 1 - b0], ra.at[c], za_s.at[c], za_r.at[c], za_dev) for c in range(nb)]
+    halve_b = [remote(sb.at[c], rb.at[c], zb_s.at[c], zb_r.at[c], zb_dev) for c in range(nb)]
+
+    def start_direct(c):
+        direct_x[c].start()
+        direct_y[c].start()
+
+    def multiply(c):
+        pass_x[c].wait_recv()
+        pass_y[c].wait_recv()
+        total = jnp.dot(
+            at[0].reshape(PLANE * chunk, rows), dp[0, c], preferred_element_type=jnp.float32
+        )
+        for p in range(1, PLANE):
+            total = total + jnp.dot(
+                at[p].reshape(PLANE * chunk, rows), dp[p, c], preferred_element_type=jnp.float32
+            )
+        for m in range(2):
+            for zz in range(2):
+                k = 2 * m + zz
+                gbuf[c, zz, m] = total[k * chunk:(k + 1) * chunk]
+        halve_a[c].start()
+
+    def reduce_a(c):
+        halve_a[c].wait_recv()
+        sb[c] = gbuf[c, b0, 1 - b1] + ra[c, 1 - b1]
+        halve_b[c].start()
+
+    def reduce_b(c):
+        halve_b[c].wait_recv()
+        grad_ref[:, c * LANES:(c + 1) * LANES] = (gbuf[c, b0, b1] + ra[c, b1]) + rb[c]
+
+    ahead = 2
+    for c in range(nb):
+        make_d_proj(c)
+        if c < ahead:
+            start_direct(c)
+
+    for r, peer_q in enumerate((xy_q, x_q, y_q)):
+        attn_copies[r].wait_recv()
+        copy = remote(at.at[peer_q, mp], at.at[peer_q, mp], p_s.at[r], p_r.at[r], partner)
+        copy.start()
+        partner_copies.append(copy)
+
+    for j in range(nf):
+        cols = slice(j * fw, (j + 1) * fw)
+        for s in range(samples):
+            gg_ref[s:s + 1, cols] = coef[s] * gate_sums[j][s]
+    loss_pair.wait_recv()
+    lbuf[d] = lpart[0] + lpart[1]
+    loss_copies = []
+    for k in range(1, n):
+        copy = remote(lbuf.at[d], lbuf.at[d], l_s.at[k], l_r.at[k], (lax.rem(d + k, n), mp))
+        copy.start()
+        loss_copies.append(copy)
+
+    for step in range(nb + 3):
+        if step < nb:
+            direct_x[step].wait_recv()
+            pass_y[step].start()
+            direct_y[step].wait_recv()
+            pass_x[step].start()
+            if step + ahead < nb:
+                start_direct(step + ahead)
+        if step == 1:
+            for copy in partner_copies:
+                copy.wait_recv()
+        if 1 <= step <= nb:
+            multiply(step - 1)
+        if 2 <= step <= nb + 1:
+            reduce_a(step - 2)
+        if 3 <= step:
+            reduce_b(step - 3)
+
+    for copy in loss_copies:
+        copy.wait_recv()
+    sums = lbuf[0]
+    for k in range(1, n):
+        sums = sums + lbuf[k]
+    loss_ref[...] = (weights * sums / floored)[0:1]
+
+    for group in (
+        count_copies, attn_copies, partner_copies, part_copies, [loss_pair], loss_copies,
+        direct_x, direct_y, pass_x, pass_y, halve_a, halve_b,
+    ):
+        for copy in group:
+            copy.wait_send()
+
+
+def fused(n, attn, w_out, resid, target, gate, bins):
+    rows, own_cols = attn.shape
+    samples = bins.shape[0]
+    full_width = w_out.shape[1]
+    chunk = full_width // n
+    nb = own_cols // LANES
+    fw = 2 * LANES if own_cols % (2 * LANES) == 0 else LANES
+    nf = own_cols // fw
+    f32, bf16 = jnp.float32, jnp.bfloat16
+    V = pltpu.VMEM
+    dma = pltpu.SemaphoreType.DMA
+    grad, gate_grad, loss = pl.pallas_call(
+        functools.partial(fused_kernel, n, full_width),
+        out_shape=(
+            jax.ShapeDtypeStruct((chunk, own_cols), f32),
+            jax.ShapeDtypeStruct((samples, own_cols), f32),
+            jax.ShapeDtypeStruct((1, NBINS), f32),
+        ),
+        in_specs=[pl.BlockSpec(memory_space=pl.ANY)] * 4
+        + [pl.BlockSpec(memory_space=pltpu.VMEM), pl.BlockSpec(memory_space=pltpu.SMEM)],
+        out_specs=(pl.BlockSpec(memory_space=pltpu.VMEM),) * 3,
+        scratch_shapes=[
+            V((rows, own_cols), bf16),
+            V((2, w_out.shape[0], own_cols), bf16),
+            V((rows, own_cols), bf16),
+            V((rows, own_cols), bf16),
+            V((rows, own_cols), f32),
+            V((nf, rows, fw), f32),
+            V((nf, rows, fw), f32),
+            V((PLANE, 2 * chunk, rows), bf16),
+            V((PLANE, 2, 2 * chunk, rows), bf16),
+            V((PLANE, nb, rows, LANES), bf16),
+            V((nb, 2, 2, chunk, LANES), f32),
+            V((nb, 2, chunk, LANES), f32),
+            V((nb, chunk, LANES), f32),
+            V((nb, chunk, LANES), f32),
+            V((n, 8, LANES), f32),
+            V((2, 8, LANES), f32),
+            V((n, 8, LANES), f32),
+            dma((5,)),
+            dma((nf,)), dma((nf,)),
+            dma((3,)), dma((3,)),
+            dma((4,)), dma((4,)),
+            dma((n,)), dma((n,)),
+            dma((n,)), dma((n,)),
+            dma((1,)), dma((1,)),
+        ] + [dma((nb,))] * 12,
+        compiler_params=pltpu.CompilerParams(collective_id=0, has_side_effects=True),
+    )(attn, w_out, resid, target, gate, bins)
+    return grad, gate_grad, loss.reshape(NBINS)
+
+
 def solution(mesh):
+    n, pair = mesh.shape["dp"], mesh.shape["mp"]
+
+    def body(attn, w_out, resid, target, gate, bins):
+        full_width = w_out.shape[1]
+        fits = (
+            pair == 2 and n == PLANE * 4 and NBINS == LANES
+            and full_width % (16 * n) == 0 and attn.shape[1] % LANES == 0
+            and attn.shape[0] % (16 * bins.shape[0]) == 0 and attn.shape[0] % LANES == 0
+        )
+        if fits:
+            return fused(n, attn, w_out, resid, target, gate, bins)
+        return shards(attn, w_out, resid, target, gate, bins)
+
     return jax.shard_map(
-        shards,
+        body,
         mesh=mesh,
         in_specs=(
             P("dp", "mp"),

time: 214 us -> 53.8 us (0.25)
  waiting for transfers between devices: 94.3 us -> 0 us
  blocking collectives: 81.4 us -> 0 us
  Pallas kernels: 0 us -> 48.6 us
  between operations: 13.8 us -> 0.64 us
  matrix products: 8.55 us -> 0 us
  other arithmetic: 7.99 us -> 0 us
  local copies, waits for them, and re-layouts: 7.85 us -> 4.19 us
    unnamed x4 -> x0, waiting for transfers between devices: 94.3 us -> none
    psum x2 -> x0, blocking collectives: 81.4 us -> none  [the longest x1 43.5 us: shards(): counts = lax.psum(local_counts, 'dp')]
    pallas_call x0 -> x1, Pallas kernels: none -> 48.6 us  [fused(): pl.pallas_call(functools.partial(fused_kernel, n, full_width), out_shape=...]
    dot_general x2 -> x0, matrix products: 8.55 us -> none  [the longest x1 4.99 us: shards(): lax.dot_general(whole_attn, d_proj, (((0,), (0,)), ((), ())), preferred_e...]
    reduce_sum x5 -> x0, other arithmetic: 5.11 us -> none  [the longest x1 2.22 us: shards(): grad_gate = jnp.sum(d_hidden * proj_cube, axis=1)]
    unnamed x17 -> x3, local copies, waits for them, and re-layouts: 7.78 us -> 4.19 us
  transfers between devices with their start and end apart: 3 -> 0, of which waited for: 1 -> 0; matrix products, arithmetic and copies ran while one was open for 4% -> 0% of each run, Pallas kernels for 0% -> 0%
where the time goes in v1:
time: 53.8 us; the launch traced here: 53.4 us
  Pallas kernels  48.6 us (90%)
  local copies, waits for them, and re-layouts  4.19 us (8%)
  between operations  0.64 us (1%)
    pallas_call x1, Pallas kernels, fused(): pl.pallas_call(functools.partial(fused_kernel, n, full_width), out_shape=...  48.6 us
    unnamed x3, local copies, waits for them, and re-layouts  4.19 us

profile of v1, /device:TPU:0, one launch (start us, length us, event | category | flops | bytes accessed | tf_op | source)
XLA Modules:
  0.0 53.4 jit_solution(8965743254703040663)
XLA Ops:
  0.6 48.6 %shard_map.85 = (f32[96,768]{1,0:T(8,128)}, f32[3,768]{1,0:T(4,128)}, f32[1,128]{1,0:T(1,128)}) custom-call(bf16[384,768]{1,0:T(8,128)(2,1)} %attn_h.1, bf16[768,1536]{1,0:T(8,128)(2,1)} %w_h.1, bf16[384,768]{1,0:T(8,128)(2,1)} %resid_h.1, bf16[384,768]{1,0:T(8,128)(2,1)} %target_h.1, f32[3,768]{1,0:T(4,128)} %gate_ref.1, s32[3]{0:T(128)} %bins_ref.1), custom_call_target="tpu_custom_call" | custom-call | tf_op jit(solution)/shard_map/pallas_call | solution.py:322
  49.2 1.7 %copy.12 = f32[96,768]{1,0:T(8,128)} copy(f32[96,768]{1,0:T(8,128)} %get-tuple-element.12) | data formatting | bytes 589824
  50.9 1.3 %copy.13 = f32[3,768]{1,0:T(4,128)} copy(f32[3,768]{1,0:T(4,128)} %get-tuple-element.13) | data formatting | bytes 18432
  52.2 1.2 %copy.14 = f32[128]{0:T(128)} copy(f32[128]{0:T(128)} %bitcast.1) | data formatting | bytes 1024

commit v2 on v1

--- a/solution.py
+++ b/solution.py
@@ -64,12 +64,12 @@
 
 def fused_kernel(
     n, full_width,
-    attn_h, w_h, resid_h, target_h, gate_ref, bins_ref,
+    attn_h, w_h, resid_h, target_h, gate_h, bins_h,
     grad_ref, gg_ref, loss_ref,
-    attn_v, w_v, resid_v, target_v, err, psend, precv,
-    at_send, at, dp, gbuf, ra, sb, rb, cnt, lpart, lbuf,
+    attn_v, w_v, resid_v, target_v, gate_ref, bins_ref, err, psend, precv,
+    at_send, at, dp, gbuf, ra, sb, rb, lpart, cnt, cline, lbuf, lline,
     ld, fs, fr, a_s, a_r, p_s, p_r, c_s, c_r, l_s, l_r, lp_s, lp_r,
-    dx_s, dx_r, dy_s, dy_r, fx_s, fx_r, fy_s, fy_r, za_s, za_r, zb_s, zb_r,
+    dx_s, dx_r, dy_s, dy_r, fx_s, fx_r, fy_s, fy_r, za_s, za_r, zk_s, zk_r, zb_s, zb_r,
 ):
     d = lax.axis_index("dp")
     mp = lax.axis_index("mp")
@@ -110,21 +110,24 @@
         pltpu.make_async_copy(own_half(mp), w_v.at[1], ld.at[2]),
         pltpu.make_async_copy(resid_h, resid_v, ld.at[3]),
         pltpu.make_async_copy(target_h, target_v, ld.at[4]),
-    ]
+        pltpu.make_async_copy(bins_h, bins_ref, ld.at[5]),
+        pltpu.make_async_copy(gate_h, gate_ref, ld.at[6]),
+    ]
+
+    barrier = pltpu.get_barrier_semaphore()
+    peers = (zb_dev, xy_dev, za_dev, x_dev, y_dev, partner)
+    for peer in peers:
+        pl.semaphore_signal(barrier, inc=1, device_id=peer, device_id_type=MESH)
+
     for load in loads:
         load.start()
-
-    barrier = pltpu.get_barrier_semaphore()
-    for k in range(1, n):
-        pl.semaphore_signal(barrier, inc=1, device_id=(lax.rem(d + k, n), mp), device_id_type=MESH)
-    pl.semaphore_signal(barrier, inc=1, device_id=partner, device_id_type=MESH)
-
+    loads[5].wait()
     lane = lax.broadcasted_iota(jnp.int32, (8, LANES), 1)
     one_hot = [(lane == bins_ref[s]).astype(jnp.float32) for s in range(samples)]
     counts_own = one_hot[0]
     for s in range(1, samples):
         counts_own = counts_own + one_hot[s]
-    cnt[d] = counts_own
+    cnt[q] = counts_own
 
     loads[0].wait()
     turned = attn_v[...].T
@@ -132,11 +135,12 @@
         zz, to = k // PLANE, k % PLANE
         at_send[to, zz * chunk:(zz + 1) * chunk, :] = turned[k * chunk:(k + 1) * chunk]
 
-    pl.semaphore_wait(barrier, n)
+    pl.semaphore_wait(barrier, len(peers))
 
     count_copies = []
-    for k in range(1, n):
-        copy = remote(cnt.at[d], cnt.at[d], c_s.at[k], c_r.at[k], (lax.rem(d + k, n), mp))
+    plane = (xy_dev, x_dev, y_dev)
+    for r, dev in enumerate(plane):
+        copy = remote(cnt.at[q], cnt.at[q], c_s.at[r], c_r.at[r], dev)
         copy.start()
         count_copies.append(copy)
     attn_copies = []
@@ -156,9 +160,18 @@
         copy = remote(psend.at[j], precv.at[j], fs.at[j], fr.at[j], partner)
         copy.start()
         part_copies.append(copy)
-    loads[2].wait()
-    loads[3].wait()
-    loads[4].wait()
+    def line_step(copies, line, values, sends, recvs, stage, dev):
+        line[2 * stage] = values
+        copy = remote(line.at[2 * stage], line.at[2 * stage + 1], sends.at[3 + stage], recvs.at[3 + stage], dev)
+        copy.start()
+        copies.append(copy)
+
+    for copy in count_copies:
+        copy.wait_recv()
+    line_step(count_copies, cline, (cnt[0] + cnt[1]) + (cnt[2] + cnt[3]), c_s, c_r, 0, za_dev)
+    for load in loads[2:5]:
+        load.wait()
+    loads[6].wait()
     square = [jnp.zeros((1, fw), jnp.float32) for _ in range(samples)]
     gate_sums = []
     for j in range(nf):
@@ -176,6 +189,9 @@
             square[s] = square[s] + jnp.sum(error * error, axis=0, keepdims=True)
             sums.append(jnp.sum(error * proj, axis=0, keepdims=True))
         gate_sums.append(sums)
+        if j == 0:
+            count_copies[3].wait_recv()
+            line_step(count_copies, cline, cline[0] + cline[1], c_s, c_r, 1, zb_dev)
 
     bin_part = jnp.zeros((8, LANES), jnp.float32)
     for s in range(samples):
@@ -189,11 +205,8 @@
     logit = jnp.log(centre) - jnp.log(1.0 - centre)
     weights = jnp.exp(-0.5 * logit * logit) / (math.sqrt(2.0 * math.pi) * centre * (1.0 - centre))
 
-    for copy in count_copies:
-        copy.wait_recv()
-    counts = cnt[0]
-    for k in range(1, n):
-        counts = counts + cnt[k]
+    count_copies[4].wait_recv()
+    counts = cline[2] + cline[3]
     floored = jnp.maximum(counts, 1.0)
     scale_bin = LOSS_SCALE * weights / floored
     coef = [
@@ -219,7 +232,12 @@
         remote(dp.at[y_q, c, second], dp.at[y_q, c, second], fx_s.at[c], fx_r.at[c], x_dev)
         for c in range(nb)
     ]
-    halve_a = [remote(gbuf.at[c, 1 - b0], ra.at[c], za_s.at[c], za_r.at[c], za_dev) for c in range(nb)]
+    halve_a = [
+        remote(gbuf.at[c, 1 - b0, 1 - b1], ra.at[c, 0], za_s.at[c], za_r.at[c], za_dev) for c in range(nb)
+    ]
+    halve_k = [
+        remote(gbuf.at[c, 1 - b0, b1], ra.at[c, 1], zk_s.at[c], zk_r.at[c], za_dev) for c in range(nb)
+    ]
     halve_b = [remote(sb.at[c], rb.at[c], zb_s.at[c], zb_r.at[c], zb_dev) for c in range(nb)]
 
     def start_direct(c):
@@ -241,15 +259,17 @@
                 k = 2 * m + zz
                 gbuf[c, zz, m] = total[k * chunk:(k + 1) * chunk]
         halve_a[c].start()
+        halve_k[c].start()
 
     def reduce_a(c):
         halve_a[c].wait_recv()
-        sb[c] = gbuf[c, b0, 1 - b1] + ra[c, 1 - b1]
+        sb[c] = gbuf[c, b0, 1 - b1] + ra[c, 0]
         halve_b[c].start()
 
     def reduce_b(c):
+        halve_k[c].wait_recv()
         halve_b[c].wait_recv()
-        grad_ref[:, c * LANES:(c + 1) * LANES] = (gbuf[c, b0, b1] + ra[c, b1]) + rb[c]
+        grad_ref[:, c * LANES:(c + 1) * LANES] = (gbuf[c, b0, b1] + ra[c, 1]) + rb[c]
 
     ahead = 2
     for c in range(nb):
@@ -268,10 +288,10 @@
         for s in range(samples):
             gg_ref[s:s + 1, cols] = coef[s] * gate_sums[j][s]
     loss_pair.wait_recv()
-    lbuf[d] = lpart[0] + lpart[1]
+    lbuf[q] = lpart[0] + lpart[1]
     loss_copies = []
-    for k in range(1, n):
-        copy = remote(lbuf.at[d], lbuf.at[d], l_s.at[k], l_r.at[k], (lax.rem(d + k, n), mp))
+    for r, dev in enumerate(plane):
+        copy = remote(lbuf.at[q], lbuf.at[q], l_s.at[r], l_r.at[r], dev)
         copy.start()
         loss_copies.append(copy)
 
@@ -288,21 +308,25 @@
                 copy.wait_recv()
         if 1 <= step <= nb:
             multiply(step - 1)
+        if step == 2:
+            for copy in loss_copies:
+                copy.wait_recv()
+            line_step(loss_copies, lline, (lbuf[0] + lbuf[1]) + (lbuf[2] + lbuf[3]), l_s, l_r, 0, za_dev)
+        if step == 4:
+            loss_copies[3].wait_recv()
+            line_step(loss_copies, lline, lline[0] + lline[1], l_s, l_r, 1, zb_dev)
         if 2 <= step <= nb + 1:
             reduce_a(step - 2)
         if 3 <= step:
             reduce_b(step - 3)
 
-    for copy in loss_copies:
-        copy.wait_recv()
-    sums = lbuf[0]
-    for k in range(1, n):
-        sums = sums + lbuf[k]
+    loss_copies[4].wait_recv()
+    sums = lline[2] + lline[3]
     loss_ref[...] = (weights * sums / floored)[0:1]
 
     for group in (
         count_copies, attn_copies, partner_copies, part_copies, [loss_pair], loss_copies,
-        direct_x, direct_y, pass_x, pass_y, halve_a, halve_b,
+        direct_x, direct_y, pass_x, pass_y, halve_a, halve_k, halve_b,
     ):
         for copy in group:
             copy.wait_send()
@@ -326,14 +350,15 @@
             jax.ShapeDtypeStruct((samples, own_cols), f32),
             jax.ShapeDtypeStruct((1, NBINS), f32),
         ),
-        in_specs=[pl.BlockSpec(memory_space=pl.ANY)] * 4
-        + [pl.BlockSpec(memory_space=pltpu.VMEM), pl.BlockSpec(memory_space=pltpu.SMEM)],
+        in_specs=[pl.BlockSpec(memory_space=pl.ANY)] * 6,
         out_specs=(pl.BlockSpec(memory_space=pltpu.VMEM),) * 3,
         scratch_shapes=[
             V((rows, own_cols), bf16),
             V((2, w_out.shape[0], own_cols), bf16),
             V((rows, own_cols), bf16),
             V((rows, own_cols), bf16),
+            V((samples, own_cols), f32),
+            pltpu.SMEM((samples,), jnp.int32),
             V((rows, own_cols), f32),
             V((nf, rows, fw), f32),
             V((nf, rows, fw), f32),
@@ -344,17 +369,19 @@
             V((nb, 2, chunk, LANES), f32),
             V((nb, chunk, LANES), f32),
             V((nb, chunk, LANES), f32),
-            V((n, 8, LANES), f32),
             V((2, 8, LANES), f32),
-            V((n, 8, LANES), f32),
-            dma((5,)),
+            V((PLANE, 8, LANES), f32),
+            V((PLANE, 8, LANES), f32),
+            V((PLANE, 8, LANES), f32),
+            V((PLANE, 8, LANES), f32),
+            dma((7,)),
             dma((nf,)), dma((nf,)),
             dma((3,)), dma((3,)),
             dma((4,)), dma((4,)),
-            dma((n,)), dma((n,)),
-            dma((n,)), dma((n,)),
+            dma((5,)), dma((5,)),
+            dma((5,)), dma((5,)),
             dma((1,)), dma((1,)),
-        ] + [dma((nb,))] * 12,
+        ] + [dma((nb,))] * 14,
         compiler_params=pltpu.CompilerParams(collective_id=0, has_side_effects=True),
     )(attn, w_out, resid, target, gate, bins)
     return grad, gate_grad, loss.reshape(NBINS)

time: 53.8 us -> 52.9 us (0.983)
  Pallas kernels: 48.6 us -> 47.8 us
    pallas_call x1, Pallas kernels: 48.6 us -> 47.8 us  [fused(): pl.pallas_call(functools.partial(fused_kernel, n, full_width), out_shape=...]
where the time goes in v2:
time: 52.9 us; the launch traced here: 52.7 us
  Pallas kernels  47.8 us (90%)
  local copies, waits for them, and re-layouts  4.19 us (8%)
  between operations  0.64 us (1%)
    pallas_call x1, Pallas kernels, fused(): pl.pallas_call(functools.partial(fused_kernel, n, full_width), out_shape=...  47.8 us
    unnamed x3, local copies, waits for them, and re-layouts  4.19 us

profile of v2, /device:TPU:0, one launch (start us, length us, event | category | flops | bytes accessed | tf_op | source)
XLA Modules:
  0.0 52.7 jit_solution(14758103039960230636)
XLA Ops:
  0.6 47.8 %shard_map.85 = (f32[96,768]{1,0:T(8,128)}, f32[3,768]{1,0:T(4,128)}, f32[1,128]{1,0:T(1,128)}) custom-call(bf16[384,768]{1,0:T(8,128)(2,1)} %attn_h.1, bf16[768,1536]{1,0:T(8,128)(2,1)} %w_h.1, bf16[384,768]{1,0:T(8,128)(2,1)} %resid_h.1, bf16[384,768]{1,0:T(8,128)(2,1)} %target_h.1, f32[3,768]{1,0:T(4,128)} %gate_h.1, s32[3]{0:T(128)} %bins_h.1), custom_call_target="tpu_custom_call" | custom-call | tf_op jit(solution)/shard_map/pallas_call | solution.py:346
  48.5 1.7 %copy.12 = f32[96,768]{1,0:T(8,128)} copy(f32[96,768]{1,0:T(8,128)} %get-tuple-element.12) | data formatting | bytes 589824
  50.2 1.3 %copy.13 = f32[3,768]{1,0:T(4,128)} copy(f32[3,768]{1,0:T(4,128)} %get-tuple-element.13) | data formatting | bytes 18432
  51.5 1.2 %copy.14 = f32[128]{0:T(128)} copy(f32[128]{0:T(128)} %bitcast.1) | data formatting | bytes 1024

commit v3 on v2

--- a/solution.py
+++ b/solution.py
@@ -66,7 +66,7 @@
     n, full_width,
     attn_h, w_h, resid_h, target_h, gate_h, bins_h,
     grad_ref, gg_ref, loss_ref,
-    attn_v, w_v, resid_v, target_v, gate_ref, bins_ref, err, psend, precv,
+    attn_v, w_v, resid_v, target_v, gate_ref, bins_ref, err, psend, precv, own_part,
     at_send, at, dp, gbuf, ra, sb, rb, lpart, cnt, cline, lbuf, lline,
     ld, fs, fr, a_s, a_r, p_s, p_r, c_s, c_r, l_s, l_r, lp_s, lp_r,
     dx_s, dx_r, dy_s, dy_r, fx_s, fx_r, fy_s, fy_r, za_s, za_r, zk_s, zk_r, zb_s, zb_r,
@@ -86,6 +86,8 @@
     x_dev, y_dev, xy_dev = (base + x_q, mp), (base + y_q, mp), (base + xy_q, mp)
     za_dev = (d + PLANE - 2 * PLANE * b0, mp)
     zb_dev = (d + 2 * PLANE - 4 * PLANE * b1, mp)
+    zab_dev = (d + PLANE - 2 * PLANE * b0 + 2 * PLANE - 4 * PLANE * b1, mp)
+    z = lax.div(d, PLANE)
     partner = (d, other)
 
     rows, own_cols = attn_v.shape
@@ -115,12 +117,12 @@
     ]
 
     barrier = pltpu.get_barrier_semaphore()
-    peers = (zb_dev, xy_dev, za_dev, x_dev, y_dev, partner)
+    peers = (zab_dev, zb_dev, xy_dev, za_dev, x_dev, y_dev, partner)
     for peer in peers:
         pl.semaphore_signal(barrier, inc=1, device_id=peer, device_id_type=MESH)
 
-    for load in loads:
-        load.start()
+    loads[0].start()
+    loads[5].start()
     loads[5].wait()
     lane = lax.broadcasted_iota(jnp.int32, (8, LANES), 1)
     one_hot = [(lane == bins_ref[s]).astype(jnp.float32) for s in range(samples)]
@@ -129,20 +131,22 @@
         counts_own = counts_own + one_hot[s]
     cnt[q] = counts_own
 
+    pl.semaphore_wait(barrier, len(peers))
+
+    count_copies = []
+    plane = (xy_dev, x_dev, y_dev)
+    for r, dev in enumerate(plane):
+        copy = remote(cnt.at[q], cnt.at[q], c_s.at[r], c_r.at[r], dev)
+        copy.start()
+        count_copies.append(copy)
     loads[0].wait()
+    for k in (1, 2, 6, 3, 4):
+        loads[k].start()
     turned = attn_v[...].T
     for k in range(own_cols // chunk):
         zz, to = k // PLANE, k % PLANE
         at_send[to, zz * chunk:(zz + 1) * chunk, :] = turned[k * chunk:(k + 1) * chunk]
 
-    pl.semaphore_wait(barrier, len(peers))
-
-    count_copies = []
-    plane = (xy_dev, x_dev, y_dev)
-    for r, dev in enumerate(plane):
-        copy = remote(cnt.at[q], cnt.at[q], c_s.at[r], c_r.at[r], dev)
-        copy.start()
-        count_copies.append(copy)
     attn_copies = []
     for r, (peer_q, dev) in enumerate(((xy_q, xy_dev), (x_q, x_dev), (y_q, y_dev))):
         copy = remote(at_send.at[peer_q], at.at[q, mp], a_s.at[r], a_r.at[r], dev)
@@ -166,22 +170,30 @@
         copy.start()
         copies.append(copy)
 
+    loads[2].wait()
+    for j in range(nf):
+        own_part[j] = jnp.dot(
+            attn_v[...], w_v[1, :, j * fw:(j + 1) * fw], preferred_element_type=jnp.float32
+        )
     for copy in count_copies:
         copy.wait_recv()
-    line_step(count_copies, cline, (cnt[0] + cnt[1]) + (cnt[2] + cnt[3]), c_s, c_r, 0, za_dev)
-    for load in loads[2:5]:
+    cline[z] = (cnt[0] + cnt[1]) + (cnt[2] + cnt[3])
+    for r, dev in enumerate((zab_dev, zb_dev, za_dev)):
+        copy = remote(cline.at[z], cline.at[z], c_s.at[3 + r], c_r.at[3 + r], dev)
+        copy.start()
+        count_copies.append(copy)
+    for load in loads[3:5]:
         load.wait()
     loads[6].wait()
     square = [jnp.zeros((1, fw), jnp.float32) for _ in range(samples)]
     gate_sums = []
     for j in range(nf):
         cols = slice(j * fw, (j + 1) * fw)
-        own = jnp.dot(attn_v[...], w_v[1, :, cols], preferred_element_type=jnp.float32)
         part_copies[j].wait_recv()
         sums = []
         for s in range(samples):
             toks = slice(s * tok, (s + 1) * tok)
-            proj = own[toks] + precv[j, toks, :]
+            proj = own_part[j, toks, :] + precv[j, toks, :]
             gate = gate_ref[s:s + 1, cols]
             hidden = resid_v[toks, cols].astype(jnp.float32) + gate * proj
             error = hidden - target_v[toks, cols].astype(jnp.float32)
@@ -189,9 +201,6 @@
             square[s] = square[s] + jnp.sum(error * error, axis=0, keepdims=True)
             sums.append(jnp.sum(error * proj, axis=0, keepdims=True))
         gate_sums.append(sums)
-        if j == 0:
-            count_copies[3].wait_recv()
-            line_step(count_copies, cline, cline[0] + cline[1], c_s, c_r, 1, zb_dev)
 
     bin_part = jnp.zeros((8, LANES), jnp.float32)
     for s in range(samples):
@@ -205,8 +214,9 @@
     logit = jnp.log(centre) - jnp.log(1.0 - centre)
     weights = jnp.exp(-0.5 * logit * logit) / (math.sqrt(2.0 * math.pi) * centre * (1.0 - centre))
 
-    count_copies[4].wait_recv()
-    counts = cline[2] + cline[3]
+    for copy in count_copies[3:]:
+        copy.wait_recv()
+    counts = (cline[0] + cline[1]) + (cline[2] + cline[3])
     floored = jnp.maximum(counts, 1.0)
     scale_bin = LOSS_SCALE * weights / floored
     coef = [
@@ -245,15 +255,15 @@
         direct_y[c].start()
 
     def multiply(c):
+        def product(p):
+            return jnp.dot(
+                at[p].reshape(PLANE * chunk, rows), dp[p, c], preferred_element_type=jnp.float32
+            )
+
+        near = product(q) + product(x_q) + product(y_q)
         pass_x[c].wait_recv()
         pass_y[c].wait_recv()
-        total = jnp.dot(
-            at[0].reshape(PLANE * chunk, rows), dp[0, c], preferred_element_type=jnp.float32
-        )
-        for p in range(1, PLANE):
-            total = total + jnp.dot(
-                at[p].reshape(PLANE * chunk, rows), dp[p, c], preferred_element_type=jnp.float32
-            )
+        total = near + product(xy_q)
         for m in range(2):
             for zz in range(2):
                 k = 2 * m + zz
@@ -330,6 +340,11 @@
     ):
         for copy in group:
             copy.wait_send()
+
+
+def hand_over(*refs):
+    for k in range(3):
+        refs[k + 3][...] = refs[k][...]
 
 
 def fused(n, attn, w_out, resid, target, gate, bins):
@@ -362,6 +377,7 @@
             V((rows, own_cols), f32),
             V((nf, rows, fw), f32),
             V((nf, rows, fw), f32),
+            V((nf, rows, fw), f32),
             V((PLANE, 2 * chunk, rows), bf16),
             V((PLANE, 2, 2 * chunk, rows), bf16),
             V((PLANE, nb, rows, LANES), bf16),
@@ -378,12 +394,19 @@
             dma((nf,)), dma((nf,)),
             dma((3,)), dma((3,)),
             dma((4,)), dma((4,)),
-            dma((5,)), dma((5,)),
+            dma((6,)), dma((6,)),
             dma((5,)), dma((5,)),
             dma((1,)), dma((1,)),
         ] + [dma((nb,))] * 14,
         compiler_params=pltpu.CompilerParams(collective_id=0, has_side_effects=True),
     )(attn, w_out, resid, target, gate, bins)
+    vmem = pl.BlockSpec(memory_space=pltpu.VMEM)
+    grad, gate_grad, loss = pl.pallas_call(
+        hand_over,
+        out_shape=tuple(jax.ShapeDtypeStruct(a.shape, f32) for a in (grad, gate_grad, loss)),
+        in_specs=[vmem] * 3,
+        out_specs=(vmem,) * 3,
+    )(grad, gate_grad, loss)
     return grad, gate_grad, loss.reshape(NBINS)
 
 

time: 52.9 us -> 48.6 us (0.919)
  local copies, waits for them, and re-layouts: 4.19 us -> 0 us
    unnamed x3 -> x0, local copies, waits for them, and re-layouts: 4.19 us -> none
    pallas_call x1, Pallas kernels: 47.8 us -> 46.1 us  [fused(): pl.pallas_call(functools.partial(fused_kernel, n, full_width), out_shape=...]
    pallas_call x0 -> x1, Pallas kernels: none -> 1.72 us  [fused(): pl.pallas_call(hand_over, out_shape=tuple((jax.ShapeDtypeStruct(a.shape,...]
where the time goes in v3:
time: 48.6 us; the launch traced here: 48.5 us
  Pallas kernels  47.8 us (98%)
  between operations  0.64 us (1%)
    pallas_call x1, Pallas kernels, fused(): pl.pallas_call(functools.partial(fused_kernel, n, full_width), out_shape=...  46.1 us
    pallas_call x1, Pallas kernels, fused(): pl.pallas_call(hand_over, out_shape=tuple((jax.ShapeDtypeStruct(a.shape,...  1.72 us

profile of v3, /device:TPU:0, one launch (start us, length us, event | category | flops | bytes accessed | tf_op | source)
XLA Modules:
  0.0 48.5 jit_solution(7008745387894031090)
XLA Ops:
  0.6 46.1 %shard_map.85 = (f32[96,768]{1,0:T(8,128)}, f32[3,768]{1,0:T(4,128)}, f32[1,128]{1,0:T(1,128)}) custom-call(bf16[384,768]{1,0:T(8,128)(2,1)} %attn_h.1, bf16[768,1536]{1,0:T(8,128)(2,1)} %w_h.1, bf16[384,768]{1,0:T(8,128)(2,1)} %resid_h.1, bf16[384,768]{1,0:T(8,128)(2,1)} %target_h.1, f32[3,768]{1,0:T(4,128)} %gate_h.1, s32[3]{0:T(128)} %bins_h.1), custom_call_target="tpu_custom_call" | custom-call | tf_op jit(solution)/shard_map/pallas_call | solution.py:361
  46.7 1.7 %shard_map.86 = (f32[96,768]{1,0:T(8,128)}, f32[3,768]{1,0:T(4,128)}, f32[1,128]{1,0:T(1,128)}) custom-call(f32[96,768]{1,0:T(8,128)} %get-tuple-element.9.refs_0_, f32[3,768]{1,0:T(4,128)} %get-tuple-element.10.refs_1_, f32[1,128]{1,0:T(1,128)} %get-tuple-element.11.refs_2_), custom_call_target="tpu_custom_call" | custom-call | tf_op jit(solution)/shard_map/pallas_call | solution.py:404

commit v4 on v3

--- a/solution.py
+++ b/solution.py
@@ -69,7 +69,7 @@
     attn_v, w_v, resid_v, target_v, gate_ref, bins_ref, err, psend, precv, own_part,
     at_send, at, dp, gbuf, ra, sb, rb, lpart, cnt, cline, lbuf, lline,
     ld, fs, fr, a_s, a_r, p_s, p_r, c_s, c_r, l_s, l_r, lp_s, lp_r,
-    dx_s, dx_r, dy_s, dy_r, fx_s, fx_r, fy_s, fy_r, za_s, za_r, zk_s, zk_r, zb_s, zb_r,
+    dx_s, dx_r, dy_s, dy_r, ex_s, ex_r, ey_s, ey_r, fx_s, fx_r, fy_s, fy_r, za_s, za_r, zk_s, zk_r, zb_s, zb_r,
 ):
     d = lax.axis_index("dp")
     mp = lax.axis_index("mp")
@@ -231,9 +231,17 @@
             d_hidden = coef[s] * err[toks, cols]
             dp[q, c, toks, :] = (d_hidden * gate_ref[s:s + 1, cols]).astype(jnp.bfloat16)
 
-    direct_x = [remote(dp.at[q, c], dp.at[q, c], dx_s.at[c], dx_r.at[c], x_dev) for c in range(nb)]
-    direct_y = [remote(dp.at[q, c], dp.at[q, c], dy_s.at[c], dy_r.at[c], y_dev) for c in range(nb)]
     first, second = pl.ds(0, half), pl.ds(half, half)
+
+    def direct(part, sends, recvs, dev):
+        return [
+            remote(dp.at[q, c, part], dp.at[q, c, part], sends.at[c], recvs.at[c], dev) for c in range(nb)
+        ]
+
+    direct_x = direct(first, dx_s, dx_r, x_dev)
+    direct_y = direct(second, dy_s, dy_r, y_dev)
+    rest_x = direct(second, ex_s, ex_r, x_dev)
+    rest_y = direct(first, ey_s, ey_r, y_dev)
     pass_y = [
         remote(dp.at[x_q, c, first], dp.at[x_q, c, first], fy_s.at[c], fy_r.at[c], y_dev)
         for c in range(nb)
@@ -253,23 +261,25 @@
     def start_direct(c):
         direct_x[c].start()
         direct_y[c].start()
+        rest_x[c].start()
+        rest_y[c].start()
 
     def multiply(c):
-        def product(p):
-            return jnp.dot(
-                at[p].reshape(PLANE * chunk, rows), dp[p, c], preferred_element_type=jnp.float32
-            )
-
-        near = product(q) + product(x_q) + product(y_q)
+        def product(p, m):
+            return jnp.dot(at[p, m], dp[p, c], preferred_element_type=jnp.float32)
+
+        halves = (1 - b1, b1)
+        near = [product(q, m) for m in halves]
+        rest_x[c].wait_recv()
+        rest_y[c].wait_recv()
+        near = [near[k] + product(x_q, m) + product(y_q, m) for k, m in enumerate(halves)]
         pass_x[c].wait_recv()
         pass_y[c].wait_recv()
-        total = near + product(xy_q)
-        for m in range(2):
+        for k, m in enumerate(halves):
+            total = near[k] + product(xy_q, m)
             for zz in range(2):
-                k = 2 * m + zz
-                gbuf[c, zz, m] = total[k * chunk:(k + 1) * chunk]
-        halve_a[c].start()
-        halve_k[c].start()
+                gbuf[c, zz, m] = total[zz * chunk:(zz + 1) * chunk]
+            (halve_a, halve_k)[k][c].start()
 
     def reduce_a(c):
         halve_a[c].wait_recv()
@@ -336,7 +346,7 @@
 
     for group in (
         count_copies, attn_copies, partner_copies, part_copies, [loss_pair], loss_copies,
-        direct_x, direct_y, pass_x, pass_y, halve_a, halve_k, halve_b,
+        direct_x, direct_y, rest_x, rest_y, pass_x, pass_y, halve_a, halve_k, halve_b,
     ):
         for copy in group:
             copy.wait_send()
@@ -397,7 +407,7 @@
             dma((6,)), dma((6,)),
             dma((5,)), dma((5,)),
             dma((1,)), dma((1,)),
-        ] + [dma((nb,))] * 14,
+        ] + [dma((nb,))] * 18,
         compiler_params=pltpu.CompilerParams(collective_id=0, has_side_effects=True),
     )(attn, w_out, resid, target, gate, bins)
     vmem = pl.BlockSpec(memory_space=pltpu.VMEM)

time: 48.6 us -> 48.1 us (0.990)
  Pallas kernels: 47.8 us -> 47.3 us
where the time goes in v4:
time: 48.1 us; the launch traced here: 48 us
  Pallas kernels  47.3 us (98%)
  between operations  0.64 us (1%)
    pallas_call x1, Pallas kernels, fused(): pl.pallas_call(functools.partial(fused_kernel, n, full_width), out_shape=...  45.6 us
    pallas_call x1, Pallas kernels, fused(): pl.pallas_call(hand_over, out_shape=tuple((jax.ShapeDtypeStruct(a.shape,...  1.72 us

profile of v4, /device:TPU:0, one launch (start us, length us, event | category | flops | bytes accessed | tf_op | source)
XLA Modules:
  0.0 48.0 jit_solution(15203860628300491782)
XLA Ops:
  0.6 45.6 %shard_map.85 = (f32[96,768]{1,0:T(8,128)}, f32[3,768]{1,0:T(4,128)}, f32[1,128]{1,0:T(1,128)}) custom-call(bf16[384,768]{1,0:T(8,128)(2,1)} %attn_h.1, bf16[768,1536]{1,0:T(8,128)(2,1)} %w_h.1, bf16[384,768]{1,0:T(8,128)(2,1)} %resid_h.1, bf16[384,768]{1,0:T(8,128)(2,1)} %target_h.1, f32[3,768]{1,0:T(4,128)} %gate_h.1, s32[3]{0:T(128)} %bins_h.1), custom_call_target="tpu_custom_call" | custom-call | tf_op jit(solution)/shard_map/pallas_call | solution.py:371
  46.3 1.7 %shard_map.86 = (f32[96,768]{1,0:T(8,128)}, f32[3,768]{1,0:T(4,128)}, f32[1,128]{1,0:T(1,128)}) custom-call(f32[96,768]{1,0:T(8,128)} %get-tuple-element.9.refs_0_, f32[3,768]{1,0:T(4,128)} %get-tuple-element.10.refs_1_, f32[1,128]{1,0:T(1,128)} %get-tuple-element.11.refs_2_), custom_call_target="tpu_custom_call" | custom-call | tf_op jit(solution)/shard_map/pallas_call | solution.py:414
